TPU v7x, 32 devices: a whole 2x2x4 slice. The times are simulated.
32 devices in a mesh: ep: 8 (over y, x, core), tp: 4 (over z).
Axes of the slice: x: 2, y: 2, z: 4, core: 2. Of those that a mesh axis runs over, the one named last changes fastest.
Arguments:
- tokens: bfloat16 [5120, 2048], P('ep'), may hold values from -6 to 6
- norm1_gain: float32 [2048], replicated, may hold values from 0.1 to 1.9
- w_qkv: bfloat16 [3, 2048, 2048], P(None, None, 'tp'), may hold values from -0.125 to 0.125
- b_qkv: bfloat16 [3, 16, 128], P(None, 'tp'), may hold values from -3 to 3
- w_out: bfloat16 [2048, 2048], P('tp'), may hold values from -1.25 to 1.25
- norm2_gain: float32 [2048], replicated, may hold values from 0.1 to 1.9
- w_router: bfloat16 [2048, 8], replicated, may hold values from -0.0625 to 0.0625
- w_sgate: bfloat16 [2048], replicated, may hold values from -0.125 to 0.125
- w_shared_gu: bfloat16 [2, 2048, 5632], P(None, None, 'tp'), may hold values from -0.125 to 0.125
- w_shared_down: bfloat16 [5632, 2048], P('tp'), may hold values from -0.15625 to 0.15625
- w_expert_gu: bfloat16 [8, 2, 2048, 1408], P('ep', None, None, 'tp'), may hold values from -0.125 to 0.125
- w_expert_down: bfloat16 [8, 1408, 2048], P('ep', 'tp'), may hold values from -0.3125 to 0.3125
- routes: int32 [5120, 4], P('ep'), may hold values from 0 to 7, all different within a row; in each aligned block of 640 rows (0 to 639, 640 to 1279, ...) at most 400 rows name the same one
- grad_out: bfloat16 [5120, 2048], P('ep'), may hold values from -6 to 6
Outputs:
- output: bfloat16 [5120, 2048], P(('ep', 'tp'))
- grad_tokens: float32 [5120, 2048], P(('ep', 'tp'))
- grad_norm1_gain: float32 [2048], P('ep')
- grad_w_qkv: float32 [3, 2048, 2048], P(None, 'ep', 'tp')
- grad_b_qkv: float32 [3, 16, 128], P(None, 'tp', 'ep')
- grad_w_out: float32 [2048, 2048], P('tp', 'ep')
- grad_norm2_gain: float32 [2048], P('ep')
- grad_w_router: float32 [2048, 8], P('ep')
- grad_w_sgate: float32 [2048], P('ep')
- grad_w_shared_gu: float32 [2, 2048, 5632], P(None, 'ep', 'tp')
- grad_w_shared_down: float32 [5632, 2048], P('tp', 'ep')
- grad_w_expert_gu: float32 [8, 2, 2048, 1408], P('ep', None, None, 'tp')
- grad_w_expert_down: float32 [8, 1408, 2048], P('ep', 'tp')
Inputs may be any that keep to these rules, and one draw needn't show every extreme that they name: `routes`: each row names 4 different experts. Among the rows of one sequence no expert is named more than 400 times, and in every draw some expert is named exactly 400 times within some sequence.
All inputs are finite; a program needn't handle non-finite values.
Results may differ from a plain program's by a relative error of at most 0.024.
Values may be sent and summed in bfloat16 or wider, within the bound.
A program may use at most 384 MiB of HBM per device.

v0:
```python
import jax
import jax.numpy as jnp
from jax import lax
from jax.sharding import PartitionSpec as P

norm_eps = 1e-06
rope_base = 1000000.0
masked_score = -1e30


def contract(left_side, right_side, left_dim, right_dim):
    return lax.dot_general(
        left_side,
        right_side,
        (((left_dim,), (right_dim,)), ((), ())),
        preferred_element_type=jnp.float32,
    )


def rms_forward(hidden, gain_vector):
    inv_scale = lax.rsqrt(jnp.mean(hidden * hidden, axis=-1, keepdims=True) + norm_eps)
    normed = hidden * inv_scale
    return (normed * gain_vector, normed, inv_scale)


def rms_backward(grad_normed_out, gain_vector, normed, inv_scale):
    grad_scaled = grad_normed_out * gain_vector
    grad_gain = jnp.sum(grad_normed_out * normed, axis=0)
    inner_mean = jnp.mean(grad_scaled * normed, axis=-1, keepdims=True)
    return (inv_scale * (grad_scaled - normed * inner_mean), grad_gain)


def rope_tables(length, head_dim):
    half_dim = head_dim // 2
    frequency = rope_base ** (-(jnp.arange(half_dim, dtype=jnp.float32) * 2.0) / head_dim)
    angles = jnp.arange(length, dtype=jnp.float32)[:, None] * frequency[None, :]
    cosine_table = jnp.concatenate([jnp.cos(angles), jnp.cos(angles)], axis=-1)[:, None, :]
    sine_table = jnp.concatenate([jnp.sin(angles), jnp.sin(angles)], axis=-1)[:, None, :]
    return (cosine_table, sine_table)


def rotate_forward(values, cosine_table, sine_table):
    half_dim = values.shape[-1] // 2
    turned = jnp.concatenate([-values[..., half_dim:], values[..., :half_dim]], axis=-1)
    return values * cosine_table + turned * sine_table


def rotate_backward(grad_rows, cosine_table, sine_table):
    half_dim = grad_rows.shape[-1] // 2
    scaled = grad_rows * sine_table
    turned = jnp.concatenate([scaled[..., half_dim:], -scaled[..., :half_dim]], axis=-1)
    return grad_rows * cosine_table + turned


def gated_backward(grad_act, gate_up):
    sigmoid_gate = jax.nn.sigmoid(gate_up[0])
    grad_gate = grad_act * gate_up[1] * sigmoid_gate * (1.0 + gate_up[0] * (1.0 - sigmoid_gate))
    grad_up = grad_act * gate_up[0] * sigmoid_gate
    return jnp.stack([grad_gate, grad_up]).astype(jnp.bfloat16)


def slot_table(routes, experts, capacity):
    pair_experts = routes.reshape(-1)
    choose = (pair_experts[:, None] == jnp.arange(experts, dtype=jnp.int32)[None, :]).astype(
        jnp.int32
    )
    before = jnp.cumsum(choose, axis=0) - choose
    slot_number = jnp.sum(before * choose, axis=1)
    slot_dest = pair_experts * capacity + slot_number
    pair_count = pair_experts.shape[0]
    slot_owner = (
        jnp.full((experts * capacity,), pair_count, jnp.int32)
        .at[slot_dest]
        .set(jnp.arange(pair_count, dtype=jnp.int32))
    )
    return (slot_dest, slot_owner)


def per_device(
    tokens,
    norm1_gain,
    w_qkv,
    b_qkv,
    w_out,
    norm2_gain,
    w_router,
    w_sgate,
    w_shared_gu,
    w_shared_down,
    w_expert_gu,
    w_expert_down,
    routes,
    grad_out,
):
    seq_rows, features = tokens.shape
    top_count = routes.shape[1]
    expert_count = w_router.shape[1]
    heads_here = b_qkv.shape[1]
    head_dim = b_qkv.shape[2]
    lane_count = lax.axis_size("tp")
    lane_index = lax.axis_index("tp")
    capacity = lane_count * (5 * seq_rows * top_count // (4 * expert_count * lane_count))
    out_rows = seq_rows // lane_count
    row_start = lane_index * out_rows
    score_scale = head_dim ** (-0.5)
    residual = tokens.astype(jnp.float32)
    normed_one, unit_one, scale_one = rms_forward(residual, norm1_gain)
    low_one = normed_one.astype(jnp.bfloat16)
    qkv_pre = jnp.einsum("ld,cde->cle", low_one, w_qkv, preferred_element_type=jnp.float32)
    qkv_pre = qkv_pre + b_qkv.reshape(3, 1, -1).astype(jnp.float32)
    cosine_table, sine_table = rope_tables(seq_rows, head_dim)
    shaped = qkv_pre.reshape(3, seq_rows, heads_here, head_dim)
    queries = rotate_forward(shaped[0], cosine_table, sine_table).astype(jnp.bfloat16)
    key_rows = rotate_forward(shaped[1], cosine_table, sine_table).astype(jnp.bfloat16)
    value_rows = shaped[2].astype(jnp.bfloat16)
    positions = jnp.arange(seq_rows)
    causal = positions[None, :] <= positions[:, None]

    def attn_scores():
        raw_scores = (
            jnp.einsum("qhd,khd->hqk", queries, key_rows, preferred_element_type=jnp.float32)
            * score_scale
        )
        return jnp.where(causal[None], raw_scores, masked_score)

    scores = attn_scores()
    score_peak = jnp.max(scores, axis=-1, keepdims=True)
    log_total = score_peak + jnp.log(jnp.sum(jnp.exp(scores - score_peak), axis=-1, keepdims=True))
    attn_probs = jnp.exp(scores - log_total).astype(jnp.bfloat16)
    attn_mixed = jnp.einsum(
        "hqk,khd->qhd", attn_probs, value_rows, preferred_element_type=jnp.float32
    )
    attn_mixed = attn_mixed.reshape(seq_rows, -1).astype(jnp.bfloat16)
    attn_total = lax.psum(jnp.dot(attn_mixed, w_out, preferred_element_type=jnp.float32), "tp")
    hidden = residual + attn_total
    normed_two, unit_two, scale_two = rms_forward(hidden, norm2_gain)
    low_two = normed_two.astype(jnp.bfloat16)
    router_probs = jax.nn.softmax(
        jnp.dot(low_two, w_router, preferred_element_type=jnp.float32), axis=-1
    )
    route_hits = (
        routes[:, :, None] == jnp.arange(expert_count, dtype=jnp.int32)[None, None, :]
    ).astype(jnp.float32)
    gate_values = jnp.sum(router_probs[:, None, :] * route_hits, axis=-1)
    shared_gate = jax.nn.sigmoid(jnp.dot(low_two, w_sgate, preferred_element_type=jnp.float32))
    shared_gu = jnp.einsum("ld,cdf->clf", low_two, w_shared_gu, preferred_element_type=jnp.float32)
    shared_act = (jax.nn.silu(shared_gu[0]) * shared_gu[1]).astype(jnp.bfloat16)
    shared_part = jnp.dot(shared_act, w_shared_down, preferred_element_type=jnp.float32)
    slot_dest, slot_owner = slot_table(routes, expert_count, capacity)
    slot_source = (slot_owner // top_count).reshape(expert_count, capacity)
    owner_table = slot_owner.reshape(expert_count, capacity)
    padded_two = jnp.concatenate([low_two, jnp.zeros((1, features), jnp.bfloat16)], axis=0)
    arrived = lax.all_to_all(padded_two[slot_source], "ep", split_axis=0, concat_axis=0, tiled=True)
    expert_in = arrived.reshape(-1, features)
    gate_up_weight = w_expert_gu[0]
    down_weight = w_expert_down[0]
    gate_up = jnp.einsum(
        "rd,cdf->crf", expert_in, gate_up_weight, preferred_element_type=jnp.float32
    )
    expert_act = (jax.nn.silu(gate_up[0]) * gate_up[1]).astype(jnp.bfloat16)
    expert_part = jnp.dot(expert_act, down_weight, preferred_element_type=jnp.float32).astype(
        jnp.bfloat16
    )
    expert_part = expert_part.reshape(expert_count, capacity, features)
    returned = lax.all_to_all(expert_part, "ep", split_axis=0, concat_axis=0, tiled=True)
    return_table = returned.reshape(-1, features)
    return_table = jnp.concatenate(
        [return_table, jnp.zeros((1, features), return_table.dtype)], axis=0
    )
    picked = return_table[slot_dest].reshape(seq_rows, top_count, features)
    expert_sum = jnp.zeros((seq_rows, features), jnp.float32)
    for route_slot in range(top_count):
        expert_sum = expert_sum + gate_values[:, route_slot, None] * picked[:, route_slot].astype(
            jnp.float32
        )
    mlp_total = lax.psum(
        (shared_gate[:, None] * shared_part + expert_sum).astype(jnp.bfloat16), "tp"
    ).astype(jnp.float32)
    output = hidden + mlp_total
    output_rows = lax.dynamic_slice_in_dim(output, row_start, out_rows, 0).astype(jnp.bfloat16)
    grad_output = grad_out.astype(jnp.float32)
    grad_sout = (shared_gate[:, None] * grad_output).astype(jnp.bfloat16)
    grad_shared_down = contract(shared_act, grad_sout, 0, 0)
    grad_sgu = gated_backward(contract(grad_sout, w_shared_down, 1, 1), shared_gu)
    grad_shared_gu = jnp.einsum(
        "ld,clf->cdf", low_two, grad_sgu, preferred_element_type=jnp.float32
    )
    grad_low_two = jnp.einsum(
        "clf,cdf->ld", grad_sgu, w_shared_gu, preferred_element_type=jnp.float32
    )
    shared_dot = jnp.sum(grad_output * shared_part, axis=-1)
    gate_dot = jnp.sum(grad_output[:, None, :] * picked.astype(jnp.float32), axis=-1)
    gate_flat = jnp.concatenate([gate_values.reshape(-1), jnp.zeros((1,), jnp.float32)])
    padded_grad = jnp.concatenate([grad_output, jnp.zeros((1, features), jnp.float32)], axis=0)
    sent_grads = (padded_grad[slot_source] * gate_flat[owner_table][:, :, None]).astype(
        jnp.bfloat16
    )
    grad_arrived = lax.all_to_all(sent_grads, "ep", split_axis=0, concat_axis=0, tiled=True)
    grad_arrived = grad_arrived.reshape(-1, features)
    grad_expert_down = contract(expert_act, grad_arrived, 0, 0)
    grad_egu = gated_backward(contract(grad_arrived, down_weight, 1, 1), gate_up)
    grad_expert_gu = jnp.einsum(
        "rd,crf->cdf", expert_in, grad_egu, preferred_element_type=jnp.float32
    )
    grad_sent = jnp.einsum(
        "crf,cdf->rd", grad_egu, gate_up_weight, preferred_element_type=jnp.float32
    ).astype(jnp.bfloat16)
    grad_returned = lax.all_to_all(
        grad_sent.reshape(expert_count, capacity, features),
        "ep",
        split_axis=0,
        concat_axis=0,
        tiled=True,
    )
    grad_pairs = grad_returned.reshape(-1, features)[slot_dest].reshape(
        seq_rows, top_count, features
    )
    grad_low_two = grad_low_two + jnp.sum(grad_pairs.astype(jnp.float32), axis=1)
    grad_low_two, gate_dot, shared_dot = (
        lax.psum(grad_low_two.astype(jnp.bfloat16), "tp").astype(jnp.float32),
        lax.psum(gate_dot.astype(jnp.bfloat16), "tp").astype(jnp.float32),
        lax.psum(shared_dot.astype(jnp.bfloat16), "tp").astype(jnp.float32),
    )
    grad_sgate_logit = (shared_dot * shared_gate * (1.0 - shared_gate)).astype(jnp.bfloat16)
    grad_sgate = contract(low_two, grad_sgate_logit, 0, 0)
    grad_probs = jnp.sum(gate_dot[:, :, None] * route_hits, axis=1)
    grad_logits = router_probs * (
        grad_probs - jnp.sum(router_probs * grad_probs, axis=-1, keepdims=True)
    )
    grad_logits = grad_logits.astype(jnp.bfloat16)
    grad_router = contract(low_two, grad_logits, 0, 0)
    grad_low_two = (
        grad_low_two
        + grad_sgate_logit.astype(jnp.float32)[:, None] * w_sgate.astype(jnp.float32)[None, :]
    )
    grad_low_two = grad_low_two + contract(grad_logits, w_router, 1, 1)
    grad_hidden_norm, grad_norm_two = rms_backward(grad_low_two, norm2_gain, unit_two, scale_two)
    grad_hidden = grad_output + grad_hidden_norm
    grad_attn = grad_hidden.astype(jnp.bfloat16)
    grad_out_weight = contract(attn_mixed, grad_attn, 0, 0)
    grad_mixed = (
        contract(grad_attn, w_out, 1, 1)
        .astype(jnp.bfloat16)
        .reshape(seq_rows, heads_here, head_dim)
    )
    again_probs = jnp.exp(attn_scores() - log_total)
    grad_values = jnp.einsum(
        "hqk,qhd->khd",
        again_probs.astype(jnp.bfloat16),
        grad_mixed,
        preferred_element_type=jnp.float32,
    )
    grad_probs_attn = jnp.einsum(
        "qhd,khd->hqk", grad_mixed, value_rows, preferred_element_type=jnp.float32
    )
    grad_scores = again_probs * (
        grad_probs_attn - jnp.sum(again_probs * grad_probs_attn, axis=-1, keepdims=True)
    )
    grad_scores = grad_scores.astype(jnp.bfloat16)
    grad_queries = (
        jnp.einsum("hqk,khd->qhd", grad_scores, key_rows, preferred_element_type=jnp.float32)
        * score_scale
    )
    grad_keys = (
        jnp.einsum("hqk,qhd->khd", grad_scores, queries, preferred_element_type=jnp.float32)
        * score_scale
    )
    grad_pre = jnp.stack(
        [
            rotate_backward(grad_queries, cosine_table, sine_table),
            rotate_backward(grad_keys, cosine_table, sine_table),
            grad_values,
        ]
    )
    grad_pre = grad_pre.reshape(3, seq_rows, -1).astype(jnp.bfloat16)
    grad_bias = jnp.sum(grad_pre.astype(jnp.float32), axis=1).reshape(3, heads_here, head_dim)
    grad_qkv = jnp.einsum("ld,cle->cde", low_one, grad_pre, preferred_element_type=jnp.float32)
    grad_low_one = lax.psum(
        jnp.einsum("cle,cde->ld", grad_pre, w_qkv, preferred_element_type=jnp.float32).astype(
            jnp.bfloat16
        ),
        "tp",
    ).astype(jnp.float32)
    grad_input_norm, grad_norm_one = rms_backward(grad_low_one, norm1_gain, unit_one, scale_one)
    grad_tokens = lax.dynamic_slice_in_dim(grad_hidden + grad_input_norm, row_start, out_rows, 0)
    summed = (
        lax.psum_scatter(grad_norm_one, "ep", scatter_dimension=0, tiled=True),
        lax.psum_scatter(grad_qkv, "ep", scatter_dimension=1, tiled=True),
        lax.psum_scatter(grad_bias, "ep", scatter_dimension=2, tiled=True),
        lax.psum_scatter(grad_out_weight, "ep", scatter_dimension=1, tiled=True),
        lax.psum_scatter(grad_norm_two, "ep", scatter_dimension=0, tiled=True),
        lax.psum_scatter(grad_router, "ep", scatter_dimension=0, tiled=True),
        lax.psum_scatter(grad_sgate, "ep", scatter_dimension=0, tiled=True),
        lax.psum_scatter(grad_shared_gu, "ep", scatter_dimension=1, tiled=True),
        lax.psum_scatter(grad_shared_down, "ep", scatter_dimension=1, tiled=True),
    )
    return (
        output_rows,
        grad_tokens,
        summed[0],
        summed[1],
        summed[2],
        summed[3],
        summed[4],
        summed[5],
        summed[6],
        summed[7],
        summed[8],
        grad_expert_gu[None],
        grad_expert_down[None],
    )


def solution(mesh):
    return jax.shard_map(
        per_device,
        mesh=mesh,
        in_specs=(
            P("ep", None),
            P(),
            P(None, None, "tp"),
            P(None, "tp", None),
            P("tp", None),
            P(),
            P(),
            P(),
            P(None, None, "tp"),
            P("tp", None),
            P("ep", None, None, "tp"),
            P("ep", "tp", None),
            P("ep", None),
            P("ep", None),
        ),
        out_specs=(
            P(("ep", "tp"), None),
            P(("ep", "tp"), None),
            P("ep"),
            P(None, "ep", "tp"),
            P(None, "tp", "ep"),
            P("tp", "ep"),
            P("ep"),
            P("ep", None),
            P("ep"),
            P(None, "ep", "tp"),
            P("tp", "ep"),
            P("ep", None, None, "tp"),
            P("ep", "tp", None),
        ),
        check_vma=False,
    )
```

profile of v0, /device:TPU:0, one launch (start us, length us, event | category | flops | bytes accessed | tf_op | source)
XLA Modules:
  0.0 1859.7 jit_solution(4364813825440306006)
XLA Ops:
  48.1 176.0 %all-reduce.13.cloned.1.call-done = f32[640,2048]{1,0:T(8,128)} async-done(((f32[640,2048]{1,0:T(8,128)}), f32[640,2048]{1,0:T(8,128)}) %all-reduce.13.cloned.1.call-update) | async-done | bytes 5242896 | tf_op jit(solution)/shard_map/psum | solution.py:134
  234.4 27.7 %gather_fusion = bf16[3200,2048]{1,0:T(8,128)(2,1)} fusion(bf16[641,2048]{1,0:T(8,128)(2,1)} %concatenate.36, s32[4096]{0:T(1024)S(1)} %pad_clamp_fusion.1), kind=kCustom, calls=%fused_computation | custom fusion | bytes 26227200 | tf_op jit(solution)/shard_map/gather | solution.py:153
  262.2 148.5 %all_to_all.20 = bf16[8,400,2048]{2,1,0:T(8,128)(2,1)S(1)} all-to-all(bf16[8,400,2048]{2,1,0:T(8,128)(2,1)} %bitcast.232), channel_id=1, replica_groups=mesh['ep'=8,'tp'=4] {'ep'}, dimensions={0} | all-to-all | bytes 26214400 | tf_op jit(solution)/shard_map/all_to_all | solution.py:153
  424.1 12.3 convolution_convert_fusion
  450.4 27.3 %gather_fusion.2 = f32[3200,2048]{1,0:T(8,128)} fusion(f32[641,2048]{1,0:T(8,128)} %concatenate.38, s32[4096]{0:T(1024)S(1)} %pad_clamp_fusion.1), kind=kCustom, calls=%fused_computation.2 | custom fusion | bytes 52441600 | tf_op jit(solution)/shard_map/gather | solution.py:195
  483.2 13.1 convolution_bitcast_fusion.3
  512.7 74.1 %all-to-all-done.1 = bf16[8,400,2048]{2,1,0:T(8,128)(2,1)} async-done(((bf16[8,400,2048]{2,1,0:T(8,128)(2,1)}), bf16[8,400,2048]{2,1,0:T(8,128)(2,1)}, u32[]{:S(2)}, u32[]{:S(2)}) %all-to-all-start.1) | async-done | bytes 13107232 | tf_op jit(solution)/shard_map/all_to_all | solution.py:165
  598.0 26.6 %gather_fusion.1 = bf16[2560,2048]{1,0:T(8,128)(2,1)} fusion(bf16[3201,2048]{1,0:T(8,128)(2,1)} %concatenate.37, s32[3072]{0:T(1024)S(1)} %pad_clamp_fusion.3), kind=kCustom, calls=%fused_computation.1 | custom fusion | bytes 20981760 | tf_op jit(solution)/shard_map/gather | solution.py:170
  624.6 16.0 reshape.304
  662.9 16.9 gather_fusion.3
  689.5 147.6 %all_to_all.21 = bf16[8,400,2048]{2,1,0:T(8,128)(2,1)S(1)} all-to-all(bf16[8,400,2048]{2,1,0:T(8,128)(2,1)S(1)} %multiply_convert_fusion), channel_id=1, replica_groups=mesh['ep'=8,'tp'=4] {'ep'}, dimensions={0} | all-to-all | bytes 26214400 | tf_op jit(solution)/shard_map/all_to_all | solution.py:198
  837.1 16.9 fusion.27
  854.1 15.2 bitcast_convert_fusion
  874.9 144.5 %all-to-all-done.3 = bf16[8,400,2048]{2,1,0:T(8,128)(2,1)} async-done(((bf16[8,400,2048]{2,1,0:T(8,128)(2,1)}), bf16[8,400,2048]{2,1,0:T(8,128)(2,1)}, u32[]{:S(2)}, u32[]{:S(2)}) %all-to-all-start.3) | async-done | bytes 13107232 | tf_op jit(solution)/shard_map/all_to_all | solution.py:208
  1019.5 27.0 %gather_fusion.4 = bf16[2560,2048]{1,0:T(8,128)(2,1)} fusion(bf16[3200,2048]{1,0:T(8,128)(2,1)} %bitcast.36, s32[3072]{0:T(1024)S(1)} %pad_clamp_fusion.2), kind=kCustom, calls=%fused_computation.4 | custom fusion | bytes 20981760 | tf_op jit(solution)/shard_map/gather | solution.py:215
  1046.5 19.0 %reshape.317 = f32[640,4,2048]{2,1,0:T(4,128)} reshape(bf16[2560,2048]{1,0:T(8,128)(2,1)} %gather_fusion.4) | data formatting | bytes 31457280 | tf_op jit(solution)/shard_map/convert_element_type | solution.py:218
  1065.5 18.5 reduce_sum.162
  1084.0 13.5 fusion.7
  1097.6 14.3 convolution_bitcast_fusion
  1113.4 31.2 %fusion.69 = (bf16[640,1,2048]{2,1,0:T(2,128)(2,1)S(1)}, bf16[640,1,2048]{2,1,0:T(2,128)(2,1)S(1)}, bf16[640,1,2048]{2,1,0:T(2,128)(2,1)S(1)}, bf16[640,1,2048]{2,1,0:T(2,128)(2,1)S(1)}) fusion(bf16[640,4,2048]{2,1,0:T(4,128)(2,1)} %reshape.304), kind=kLoop, calls=%fused_computation.195 | loop fusion | bytes 20971520 | tf_op jit(solution)/shard_map/slice | solution.py:173
  1144.7 17.1 fusion.4
  1161.8 36.8 %all-reduce.15.cloned.1.call-done = bf16[640,2048]{1,0:T(8,128)(2,1)} async-done(((bf16[640,2048]{1,0:T(8,128)(2,1)}), bf16[640,2048]{1,0:T(8,128)(2,1)}) %all-reduce.15.cloned.1.call-update) | async-done | bytes 2621456 | tf_op jit(solution)/shard_map/psum | solution.py:220
  1270.4 11.4 fusion.46
  1303.7 11.6 convolution_bitcast_fusion.4
  1315.3 32.0 %reduce-scatter.15.cloned.1.call-done = f32[2,256,1408]{1,2,0:T(8,128)} async-done(((f32[2,2048,1408]{1,2,0:T(8,128)}), f32[2,256,1408]{1,2,0:T(8,128)}) %reduce-scatter.15.cloned.1.call-update) | async-done | bytes 2883600 | tf_op jit(solution)/shard_map/reduce_scatter | solution.py:294
  1350.7 33.6 %reduce-scatter.19.cloned.1.call-done = f32[16,12]{1,0:T(8,128)} async-done(((f32[128,12]{1,0:T(8,128)}), f32[16,12]{1,0:T(8,128)}) %reduce-scatter.19.cloned.1.call-update) | async-done | bytes 784
  1385.8 189.8 %all-reduce.17.cloned.1.call-done = (bf16[640,2048]{1,0:T(8,128)(2,1)}, bf16[640,2048]{1,0:T(8,128)(2,1)}) async-done(((bf16[640,2048]{1,0:T(8,128)(2,1)}, bf16[640,2048]{1,0:T(8,128)(2,1)}), (bf16[640,2048]{1,0:T(8,128)(2,1)}, bf16[640,2048]{1,0:T(8,128)(2,1)})) %all-reduce.17.cloned.1.call-update) | async-done | bytes 5242896 | tf_op jit(solution)/shard_map/psum | solution.py:176
  1582.8 23.8 %all-reduce.6 = (f32[2048]{0:T(1024)S(1)}, f32[2048]{0:T(1024)S(1)}, f32[2048]{0:T(1024)S(1)}) all-reduce(f32[2048]{0:T(1024)S(1)} %get-tuple-element.93, f32[2048]{0:T(1024)S(1)} %copy-done.55, f32[2048]{0:T(1024)S(1)} %bitcast.256), channel_id=2, replica_groups=mesh['ep'=8,'tp'=4] {'ep'}, use_global_device_ids=true, to_apply=%region_26.27.clone | all-reduce | flops 6144 | bytes 49152
  1614.7 55.1 %reduce-scatter.9.cloned.1.call-done = f32[3,256,512]{1,2,0:T(8,128)} async-done(((f32[3,2048,512]{1,2,0:T(8,128)}), f32[3,256,512]{1,2,0:T(8,128)}) %reduce-scatter.9.cloned.1.call-update) | async-done | bytes 1572880 | tf_op jit(solution)/shard_map/reduce_scatter | solution.py:288
  1672.9 87.9 %reduce-scatter.17.cloned.1.call-done = f32[1408,256]{1,0:T(8,128)} async-done(((f32[1408,2048]{1,0:T(8,128)}), f32[1408,256]{1,0:T(8,128)}) %reduce-scatter.17.cloned.1.call-update) | async-done | bytes 1441808 | tf_op jit(solution)/shard_map/reduce_scatter | solution.py:295
  1760.8 37.1 %reduce-scatter.13.cloned.1.call-done = f32[256,8]{0,1:T(8,128)} async-done(((f32[2048,8]{0,1:T(8,128)}), f32[256,8]{0,1:T(8,128)}) %reduce-scatter.13.cloned.1.call-update) | async-done | bytes 8208 | tf_op jit(solution)/shard_map/reduce_scatter | solution.py:292
  1797.9 55.0 %reduce-scatter.11.cloned.1.call-done = f32[512,256]{1,0:T(8,128)} async-done(((f32[512,2048]{1,0:T(8,128)}), f32[512,256]{1,0:T(8,128)}) %reduce-scatter.11.cloned.1.call-update) | async-done | bytes 524304 | tf_op jit(solution)/shard_map/reduce_scatter | solution.py:290
  (295 shorter events, 265.9 us)
Async XLA Ops:
  7.2 403.5 %copy-start = (bf16[1,2,2048,352]{2,3,1,0:T(8,128)(2,1)S(1)}, bf16[1,2,2048,352]{2,3,1,0:T(8,128)(2,1)}, u32[]{:S(2)}) copy-start(bf16[1,2,2048,352]{2,3,1,0:T(8,128)(2,1)} %param.24) | copy-start | bytes 8650756
  7.2 217.0 %all-reduce.13.cloned.1.call-start = ((), (), s32[]{:S(2)}) async-start(), calls=%async_computation.10 | async-start | bytes 10485760 | tf_op jit(solution)/shard_map/psum | solution.py:134
  7.4 18.0 copy-start.14
  48.1 182.5 %copy-start.44 = (f32[2048]{0:T(1024)S(1)}, f32[2048]{0:T(1024)}, u32[]{:S(2)}) copy-start(f32[2048]{0:T(1024)} %param.19) | copy-start | bytes 24580
  436.5 150.3 %all-to-all-start.1 = ((bf16[8,400,2048]{2,1,0:T(8,128)(2,1)}), bf16[8,400,2048]{2,1,0:T(8,128)(2,1)}, u32[]{:S(2)}, u32[]{:S(2)}) async-start(bf16[8,400,2048]{2,1,0:T(8,128)(2,1)} %bitcast.239), calls=%async_computation.1 | async-start | bytes 26214400 | tf_op jit(solution)/shard_map/all_to_all | solution.py:165
  450.4 27.3 %copy-start.52 = (s32[2560]{0:T(1024)S(1)}, s32[2560]{0:T(1024)}, u32[]{:S(2)}) copy-start(s32[2560]{0:T(1024)} %get-tuple-element.95) | copy-start | bytes 30724
  450.4 27.3 %copy-start.34 = (bf16[2048,8]{0,1:T(8,128)(2,1)S(1)}, bf16[2048,8]{0,1:T(8,128)(2,1)}, u32[]{:S(2)}) copy-start(bf16[2048,8]{0,1:T(8,128)(2,1)} %param.20) | copy-start | bytes 98308
  477.7 18.6 slice-start.6
  483.0 13.3 copy-start.53
  483.1 13.2 copy-start.58
  640.6 21.2 %copy-start.41 = (s32[640,4]{0,1:T(4,128)S(1)}, s32[640,4]{0,1:T(4,128)}, u32[]{:S(2)}) copy-start(s32[640,4]{0,1:T(4,128)} %param.26) | copy-start | bytes 30724
  662.5 17.3 copy-start.42
  689.5 147.6 %copy-start.65 = (bf16[1,352,2048]{2,1,0:T(8,128)(2,1)S(1)}, bf16[1,352,2048]{2,1,0:T(8,128)(2,1)}, u32[]{:S(2)}) copy-start(bf16[1,352,2048]{2,1,0:T(8,128)(2,1)} %param.25) | copy-start | bytes 4325380
  837.1 17.0 copy-start.13
  869.3 150.2 %all-to-all-start.3 = ((bf16[8,400,2048]{2,1,0:T(8,128)(2,1)}), bf16[8,400,2048]{2,1,0:T(8,128)(2,1)}, u32[]{:S(2)}, u32[]{:S(2)}) async-start(bf16[8,400,2048]{2,1,0:T(8,128)(2,1)} %bitcast.240), calls=%async_computation.3 | async-start | bytes 26214400 | tf_op jit(solution)/shard_map/all_to_all | solution.py:208
  874.9 323.7 %all-reduce.15.cloned.1.call-start = ((), (), s32[]{:S(2)}) async-start(), calls=%async_computation.11 | async-start | bytes 5242880 | tf_op jit(solution)/shard_map/psum | solution.py:220
  1084.0 13.6 copy-start.4
  1097.5 249.8 %reduce-scatter.15.cloned.1.call-start = ((), (), s32[]{:S(2)}) async-start(), calls=%async_computation.15 | async-start | bytes 25952256 | tf_op jit(solution)/shard_map/reduce_scatter | solution.py:294
  1112.0 272.3 %reduce-scatter.19.cloned.1.call-start = ((), (), s32[]{:S(2)}) async-start(), calls=%async_computation.17 | async-start | bytes 73728
  1113.4 31.2 %copy-start.59 = (f32[640]{0:T(1024)S(1)}, f32[640]{0:T(1024)}, u32[]{:S(2)}) copy-start(f32[640]{0:T(1024)} %copy-done.58) | copy-start | bytes 7684
  1144.7 53.9 %copy-start.35 = (bf16[2048,8]{0,1:T(8,128)(2,1)S(1)}, bf16[2048,8]{0,1:T(8,128)(2,1)}, u32[]{:S(2)}) copy-start(bf16[2048,8]{0,1:T(8,128)(2,1)} %param.20) | copy-start | bytes 98308
  1144.7 53.9 %copy-start.45 = (f32[2048]{0:T(1024)S(1)}, f32[2048]{0:T(1024)}, u32[]{:S(2)}) copy-start(f32[2048]{0:T(1024)} %param.19) | copy-start | bytes 24580
  1144.7 53.9 %copy-start.49 = (f32[640]{0:T(1024)S(1)}, f32[640]{0:T(1024)}, u32[]{:S(2)}) copy-start(f32[640]{0:T(1024)} %copy-done.48) | copy-start | bytes 7684
  1198.6 21.3 %slice-start = ((s8[6553600]{0:T(1024)(128)(4,1)}), s8[4194304]{0:T(1024)(128)(4,1)S(1)}, s32[]{:S(2)}) async-start(s8[6553600]{0:T(1024)(128)(4,1)} %bitcast.229), calls=%async_computation.19 | async-start | bytes 8388608
  1250.1 325.5 %all-reduce.17.cloned.1.call-start = ((), (), s32[]{:S(2)}) async-start(), calls=%async_computation.18 | async-start | bytes 10485760 | tf_op jit(solution)/shard_map/psum | solution.py:176
  1259.1 410.7 %reduce-scatter.9.cloned.1.call-start = ((), (), s32[]{:S(2)}) async-start(), calls=%async_computation.12 | async-start | bytes 14155776 | tf_op jit(solution)/shard_map/reduce_scatter | solution.py:288
  1270.3 490.5 %reduce-scatter.17.cloned.1.call-start = ((), (), s32[]{:S(2)}) async-start(), calls=%async_computation.16 | async-start | bytes 12976128 | tf_op jit(solution)/shard_map/reduce_scatter | solution.py:295
  1281.8 516.1 %reduce-scatter.13.cloned.1.call-start = ((), (), s32[]{:S(2)}) async-start(), calls=%async_computation.14 | async-start | bytes 73728 | tf_op jit(solution)/shard_map/reduce_scatter | solution.py:292
  1283.0 570.0 %reduce-scatter.11.cloned.1.call-start = ((), (), s32[]{:S(2)}) async-start(), calls=%async_computation.13 | async-start | bytes 4718592 | tf_op jit(solution)/shard_map/reduce_scatter | solution.py:290
  1289.8 13.8 slice-start.2
  1315.3 260.2 %copy-start.8 = (bf16[640,2048]{1,0:T(8,128)(2,1)S(1)}, bf16[640,2048]{1,0:T(8,128)(2,1)}, u32[]{:S(2)}) copy-start(bf16[640,2048]{1,0:T(8,128)(2,1)} %param.14) | copy-start | bytes 7864324
  1608.6 244.3 %copy-start.1 = (bf16[1,2,2048,352]{2,3,1,0:T(8,128)(2,1)S(1)}, bf16[1,2,2048,352]{2,3,1,0:T(8,128)(2,1)}, u32[]{:S(2)}) copy-start(bf16[1,2,2048,352]{2,3,1,0:T(8,128)(2,1)} %param.24) | copy-start | bytes 8650756
  (57 other events, 273.0 us)
Sparse Core Ops, SparseCore 0:
  32.5 191.6 all-reduce.12
  1097.7 100.8 all-reduce.14
  1202.2 145.0 reduce-scatter.14
  1350.7 33.5 reduce-scatter.18
  1386.6 188.9 all-reduce.16
  1578.9 90.8 reduce-scatter.8
  1673.9 86.8 reduce-scatter.16
  1764.3 33.5 reduce-scatter.12
  1801.8 51.0 reduce-scatter.10
where the time goes:
time: 1870 us; the launch traced here: 1860 us
  waiting for transfers between devices  922 us (49%)
  blocking collectives  330 us (18%)
  local copies, waits for them, and re-layouts  254 us (14%)
  matrix products  219 us (12%)
  other arithmetic  107 us (6%)
    psum x1, waiting for transfers between devices, per_device(): lax.psum((shared_gate[:, None] * shared_part + expert_sum).astype(jnp.bfl...  190 us
    psum x1, waiting for transfers between devices, per_device(): lax.psum(jnp.dot(attn_mixed, w_out, preferred_element_type=jnp.float32),...  176 us
    all_to_all x1, blocking collectives, per_device(): lax.all_to_all(padded_two[slot_source], 'ep', split_axis=0, concat_axis=0...  149 us
    all_to_all x1, blocking collectives, per_device(): lax.all_to_all(sent_grads, 'ep', split_axis=0, concat_axis=0, tiled=True)  148 us
    all_to_all x1, waiting for transfers between devices, per_device(): lax.all_to_all(grad_sent.reshape(expert_count, capacity, features), 'ep',...  145 us
    reduce_scatter x1, waiting for transfers between devices, per_device(): lax.psum_scatter(grad_shared_down, 'ep', scatter_dimension=1, tiled=True)  87.9 us
    all_to_all x1, waiting for transfers between devices, per_device(): lax.all_to_all(expert_part, 'ep', split_axis=0, concat_axis=0, tiled=True)  74.1 us
    dot_general x9, matrix products, contract(): lax.dot_general(left_side, right_side, (((left_dim,), (right_dim,)), ((),...  70.1 us
  transfers between devices with their start and end apart: 11, of which 11 were waited for; matrix products, arithmetic and copies ran while one was open for 15% of the time, Pallas kernels for 0%

commit v1 on v0

--- a/solution.py
+++ b/solution.py
@@ -1,6 +1,10 @@
+import functools
+
 import jax
 import jax.numpy as jnp
 from jax import lax
+from jax.experimental import pallas as pl
+from jax.experimental.pallas import tpu as pltpu
 from jax.sharding import PartitionSpec as P
 
 norm_eps = 1e-06
@@ -76,7 +80,7 @@
     return (slot_dest, slot_owner)
 
 
-def per_device(
+def routed_device(
     tokens,
     norm1_gain,
     w_qkv,
@@ -311,6 +315,431 @@
     )
 
 
+def expert_weights(w_expert_gu, w_expert_down, w_shared_gu, w_shared_down, w_router, w_sgate):
+    features, experts = w_router.shape
+    groups = lax.axis_size("ep")
+    expert_units = w_expert_gu.shape[3]
+    share = w_shared_gu.shape[2] // groups
+    units = expert_units + share
+    padded = -(-(units + experts + 1) // 128) * 128
+    start = lax.axis_index("ep") * share
+    shared_gu = lax.dynamic_slice_in_dim(w_shared_gu, start, share, 2)
+    shared_down = lax.dynamic_slice_in_dim(w_shared_down, start, share, 0)
+    gate_side = jnp.concatenate(
+        [
+            w_expert_gu[0, 0],
+            shared_gu[0],
+            jnp.zeros((features, padded - units - experts - 1), jnp.bfloat16),
+            w_router,
+            w_sgate[:, None],
+        ],
+        axis=1,
+    )
+    up_side = jnp.concatenate(
+        [w_expert_gu[0, 1], shared_gu[1], jnp.zeros((features, padded - units), jnp.bfloat16)],
+        axis=1,
+    )
+    down = jnp.concatenate(
+        [w_expert_down[0], shared_down, jnp.zeros((padded - units, features), jnp.bfloat16)], axis=0
+    )
+    return gate_side, up_side, down, units
+
+
+def expert_kernel(
+    experts,
+    expert_units,
+    units,
+    index_ref,
+    rows_ref,
+    grads_ref,
+    chosen_ref,
+    gate_ref,
+    up_ref,
+    down_ref,
+    out_ref,
+    back_ref,
+    act_ref,
+    grad_gate_ref,
+    grad_up_ref,
+):
+    features = rows_ref.shape[1]
+    padded = gate_ref.shape[1]
+    expert = index_ref[0]
+    rows = rows_ref[...]
+    gate_pre = jnp.dot(rows, gate_ref[...], preferred_element_type=jnp.float32)
+    up_pre = jnp.dot(rows, up_ref[...], preferred_element_type=jnp.float32)
+    grad_down_act = contract(grads_ref[...], down_ref[...], 1, 1)
+    last = gate_pre[:, padded - 128 :]
+    lane = lax.broadcasted_iota(jnp.int32, last.shape, 1)
+    first = 127 - experts
+    routing = (lane >= first) & (lane < 127)
+    peak = jnp.max(jnp.where(routing, last, masked_score), axis=1, keepdims=True)
+    powers = jnp.where(routing, jnp.exp(last - peak), 0.0)
+    powers = jnp.where(routing, powers, 0.0)
+    own_power = jnp.sum(jnp.where(lane == first + expert, powers, 0.0), axis=1, keepdims=True)
+    expert_gate = chosen_ref[...] * own_power / jnp.sum(powers, axis=1, keepdims=True)
+    token_sgate = jax.nn.sigmoid(
+        jnp.sum(jnp.where(lane == 127, last, 0.0), axis=1, keepdims=True)
+    )
+    column = lax.broadcasted_iota(jnp.int32, gate_pre.shape, 1)
+    unit_gate = jnp.where(
+        column < expert_units, expert_gate, jnp.where(column < units, token_sgate, 0.0)
+    )
+    sigmoid_gate = jax.nn.sigmoid(gate_pre)
+    silu_gate = gate_pre * sigmoid_gate
+    act = silu_gate * up_pre
+    gated_act = (act * unit_gate).astype(jnp.bfloat16)
+    act_ref[...] = gated_act
+    dots = act * grad_down_act
+    expert_dot = jnp.sum(jnp.where(column < expert_units, dots, 0.0), axis=1, keepdims=True)
+    shared_dot = jnp.sum(
+        jnp.where((column >= expert_units) & (column < units), dots, 0.0), axis=1, keepdims=True
+    )
+    grad_act = grad_down_act * unit_gate
+    grad_gate = (
+        grad_act * up_pre * sigmoid_gate * (1.0 + gate_pre * (1.0 - sigmoid_gate))
+    ).astype(jnp.bfloat16)
+    grad_up = (grad_act * silu_gate).astype(jnp.bfloat16)
+    grad_gate_ref[...] = grad_gate
+    grad_up_ref[...] = grad_up
+    piece = 512 if features % 512 == 0 else features
+    for start in range(0, features, piece):
+        columns = pl.ds(start, piece)
+        back_ref[:, columns] = (
+            contract(grad_gate, gate_ref[columns, :], 1, 1)
+            + contract(grad_up, up_ref[columns, :], 1, 1)
+        ).astype(jnp.bfloat16)
+        out_ref[:, columns] = jnp.dot(
+            gated_act, down_ref[:, columns], preferred_element_type=jnp.float32
+        ).astype(jnp.bfloat16)
+    back_ref[:, features:] = jnp.where(
+        lane == expert, expert_dot, jnp.where(lane == experts, shared_dot, 0.0)
+    ).astype(jnp.bfloat16)
+
+
+def expert_layer(rows, grads, chosen, gate_side, up_side, down, experts, expert_units, units):
+    count, features = rows.shape
+    padded = down.shape[0]
+    block = max(size for size in range(16, 513, 16) if count % size == 0)
+    index = lax.axis_index("ep").reshape(1).astype(jnp.int32)
+
+    def moving(width):
+        return pl.BlockSpec((block, width), lambda i: (i, 0))
+
+    def held(array):
+        return pl.BlockSpec(array.shape, lambda i: (0, 0), pipeline_mode=pl.Buffered(1))
+
+    return pl.pallas_call(
+        functools.partial(expert_kernel, experts, expert_units, units),
+        grid=(count // block,),
+        in_specs=[
+            pl.BlockSpec(memory_space=pltpu.SMEM),
+            moving(features),
+            moving(features),
+            moving(1),
+            held(gate_side),
+            held(up_side),
+            held(down),
+        ],
+        out_specs=[
+            moving(features),
+            moving(features + 128),
+            moving(padded),
+            moving(padded),
+            moving(padded),
+        ],
+        out_shape=[
+            jax.ShapeDtypeStruct((count, features), jnp.bfloat16),
+            jax.ShapeDtypeStruct((count, features + 128), jnp.bfloat16),
+            jax.ShapeDtypeStruct((count, padded), jnp.bfloat16),
+            jax.ShapeDtypeStruct((count, padded), jnp.bfloat16),
+            jax.ShapeDtypeStruct((count, padded), jnp.bfloat16),
+        ],
+        compiler_params=pltpu.CompilerParams(vmem_limit_bytes=60 * 1024 * 1024),
+        cost_estimate=pl.CostEstimate(
+            flops=12 * count * features * padded,
+            bytes_accessed=8 * count * features,
+            transcendentals=count * padded,
+        ),
+    )(index, rows, grads, chosen, gate_side, up_side, down)
+
+
+def dense_device(
+    tokens,
+    norm1_gain,
+    w_qkv,
+    b_qkv,
+    w_out,
+    norm2_gain,
+    w_router,
+    w_sgate,
+    w_shared_gu,
+    w_shared_down,
+    w_expert_gu,
+    w_expert_down,
+    routes,
+    grad_out,
+):
+    seq_rows, features = tokens.shape
+    experts = w_router.shape[1]
+    heads_here = b_qkv.shape[1]
+    head_dim = b_qkv.shape[2]
+    groups = lax.axis_size("ep")
+    lanes = lax.axis_size("tp")
+    group_index = lax.axis_index("ep")
+    lane_index = lax.axis_index("tp")
+    own_rows = seq_rows // lanes
+    row_start = lane_index * own_rows
+    score_scale = head_dim ** (-0.5)
+
+    halves = 2
+    half_rows = own_rows // halves
+
+    def mine(array):
+        return lax.dynamic_slice_in_dim(array, row_start, own_rows, 0)
+
+    def part_of(array, half):
+        cut = array.reshape((lanes, halves, half_rows) + array.shape[1:])[:, half]
+        return cut.reshape((lanes * half_rows,) + array.shape[1:])
+
+    all_grads = [
+        lax.all_gather(part_of(grad_out, half), "ep", axis=0, tiled=True) for half in range(halves)
+    ]
+    all_routes = lax.all_gather(routes, "ep", axis=0, tiled=True)
+    chosen = jnp.sum((all_routes == group_index).astype(jnp.float32), axis=1, keepdims=True)
+    chosen = chosen.reshape(groups, lanes, halves, half_rows)
+
+    residual = tokens.astype(jnp.float32)
+    normed_one, unit_one, scale_one = rms_forward(residual, norm1_gain)
+    low_one = normed_one.astype(jnp.bfloat16)
+    qkv_pre = jnp.einsum("ld,cde->cle", low_one, w_qkv, preferred_element_type=jnp.float32)
+    qkv_pre = qkv_pre + b_qkv.reshape(3, 1, -1).astype(jnp.float32)
+    cosine_table, sine_table = rope_tables(seq_rows, head_dim)
+    shaped = qkv_pre.reshape(3, seq_rows, heads_here, head_dim)
+    queries = rotate_forward(shaped[0], cosine_table, sine_table).astype(jnp.bfloat16)
+    key_rows = rotate_forward(shaped[1], cosine_table, sine_table).astype(jnp.bfloat16)
+    value_rows = shaped[2].astype(jnp.bfloat16)
+    positions = jnp.arange(seq_rows)
+    causal = positions[None, :] <= positions[:, None]
+
+    def attn_scores():
+        raw_scores = (
+            jnp.einsum("qhd,khd->hqk", queries, key_rows, preferred_element_type=jnp.float32)
+            * score_scale
+        )
+        return jnp.where(causal[None], raw_scores, masked_score)
+
+    scores = attn_scores()
+    score_peak = jnp.max(scores, axis=-1, keepdims=True)
+    log_total = score_peak + jnp.log(jnp.sum(jnp.exp(scores - score_peak), axis=-1, keepdims=True))
+    attn_probs = jnp.exp(scores - log_total).astype(jnp.bfloat16)
+    attn_mixed = jnp.einsum(
+        "hqk,khd->qhd", attn_probs, value_rows, preferred_element_type=jnp.float32
+    )
+    attn_mixed = attn_mixed.reshape(seq_rows, -1).astype(jnp.bfloat16)
+    attn_part = jnp.dot(attn_mixed, w_out, preferred_element_type=jnp.float32)
+    attn_part = attn_part.astype(jnp.bfloat16)
+    gate_side, up_side, down, units = expert_weights(
+        w_expert_gu, w_expert_down, w_shared_gu, w_shared_down, w_router, w_sgate
+    )
+    expert_units = w_expert_gu.shape[3]
+    own_tokens = mine(tokens)
+    own_grads = mine(grad_out).astype(jnp.float32)
+    own_hits = jnp.sum(
+        (mine(routes)[:, :, None] == jnp.arange(experts, dtype=jnp.int32)[None, None, :]).astype(
+            jnp.float32
+        ),
+        axis=1,
+    )
+
+    rows_of, kept, layer = [], [], []
+    for half in range(halves):
+        here = slice(half * half_rows, (half + 1) * half_rows)
+        attn_total = lax.psum_scatter(
+            part_of(attn_part, half), "tp", scatter_dimension=0, tiled=True
+        )
+        hidden = own_tokens[here].astype(jnp.float32) + attn_total.astype(jnp.float32)
+        normed_two, unit_two, scale_two = rms_forward(hidden, norm2_gain)
+        low_two = normed_two.astype(jnp.bfloat16)
+        rows_of.append(lax.all_gather(low_two, ("ep", "tp"), axis=0, tiled=True))
+        kept.append((hidden, unit_two, scale_two, low_two))
+    for half in range(halves):
+        layer.append(
+            expert_layer(
+                rows_of[half],
+                all_grads[half],
+                chosen[:, :, half].reshape(-1, 1),
+                gate_side,
+                up_side,
+                down,
+                experts,
+                expert_units,
+                units,
+            )
+        )
+
+    grad_hidden, gathered, small_sums, back_sums = [], [], [], []
+    for half in range(halves):
+        here = slice(half * half_rows, (half + 1) * half_rows)
+        hidden, unit_two, scale_two, low_two = kept[half]
+        grad_sum = lax.psum_scatter(layer[half][1], "ep", scatter_dimension=0, tiled=True)
+        back_sums.append(grad_sum)
+        grad_sum = lax.psum_scatter(grad_sum, "tp", scatter_dimension=0, tiled=True)
+        grad_sum = grad_sum.astype(jnp.float32)
+        router_probs = jax.nn.softmax(
+            jnp.dot(low_two, w_router, preferred_element_type=jnp.float32), axis=-1
+        )
+        shared_gate = jax.nn.sigmoid(
+            jnp.dot(low_two, w_sgate, preferred_element_type=jnp.float32)
+        )
+        grad_probs = grad_sum[:, features : features + experts] * own_hits[here]
+        own_sdot = grad_sum[:, features + experts]
+        grad_sgate_logit = (own_sdot * shared_gate * (1.0 - shared_gate)).astype(jnp.bfloat16)
+        grad_logits = router_probs * (
+            grad_probs - jnp.sum(router_probs * grad_probs, axis=-1, keepdims=True)
+        )
+        grad_logits = grad_logits.astype(jnp.bfloat16)
+        grad_low_two = (
+            grad_sum[:, :features]
+            + grad_sgate_logit.astype(jnp.float32)[:, None] * w_sgate.astype(jnp.float32)[None, :]
+            + contract(grad_logits, w_router, 1, 1)
+        )
+        grad_hidden_norm, grad_norm_two = rms_backward(
+            grad_low_two, norm2_gain, unit_two, scale_two
+        )
+        grad_hidden.append(own_grads[here] + grad_hidden_norm)
+        gathered.append(
+            lax.all_gather(grad_hidden[half].astype(jnp.bfloat16), "tp", axis=0, tiled=True)
+        )
+        grad_router = contract(low_two, grad_logits, 0, 0)
+        grad_sgate = contract(low_two, grad_sgate_logit, 0, 0)
+        small_sums.append(
+            jnp.concatenate([grad_norm_two[None], grad_sgate[None], grad_router.T], axis=0)
+        )
+    grad_hidden = jnp.concatenate(grad_hidden, axis=0)
+    grad_attn = jnp.stack(
+        [piece.reshape(lanes, half_rows, features) for piece in gathered], axis=1
+    ).reshape(seq_rows, features)
+
+    output_rows = []
+    for half in range(halves):
+        out_part, _ = lax.optimization_barrier((layer[half][0], back_sums[-1]))
+        out_sum = lax.psum_scatter(out_part, "ep", scatter_dimension=0, tiled=True)
+        out_sum = lax.psum_scatter(out_sum, "tp", scatter_dimension=0, tiled=True)
+        output_rows.append((kept[half][0] + out_sum.astype(jnp.float32)).astype(jnp.bfloat16))
+    output_rows = jnp.concatenate(output_rows, axis=0)
+
+    def over_rows(left, right):
+        return functools.reduce(
+            jnp.add, [contract(left[half], right[half], 0, 0) for half in range(halves)]
+        )
+
+    grad_gate_weight = over_rows(rows_of, [results[3] for results in layer])
+    grad_up_weight = over_rows(rows_of, [results[4] for results in layer])
+    grad_down_weight = over_rows([results[2] for results in layer], all_grads)
+    grad_expert_gu = jnp.stack(
+        [grad_gate_weight[:, :expert_units], grad_up_weight[:, :expert_units]]
+    )
+    grad_expert_down = grad_down_weight[:expert_units]
+    share = units - expert_units
+    sent_shared = jnp.concatenate(
+        [
+            grad_gate_weight[:, expert_units:units],
+            grad_up_weight[:, expert_units:units],
+            grad_down_weight[expert_units:units].T,
+        ],
+        axis=1,
+    ).astype(jnp.bfloat16)
+    got_shared = lax.all_to_all(
+        sent_shared.reshape(groups, features // groups, 3 * share), "ep", 0, 0, tiled=True
+    ).astype(jnp.float32)
+    got_shared = got_shared.reshape(groups, features // groups, 3, share)
+    grad_shared_gu = jnp.transpose(got_shared[:, :, :2], (2, 1, 0, 3)).reshape(
+        2, features // groups, groups * share
+    )
+    grad_shared_down = jnp.transpose(got_shared[:, :, 2], (0, 2, 1)).reshape(
+        groups * share, features // groups
+    )
+
+    grad_mixed = (
+        contract(grad_attn, w_out, 1, 1)
+        .astype(jnp.bfloat16)
+        .reshape(seq_rows, heads_here, head_dim)
+    )
+    again_probs = jnp.exp(attn_scores() - log_total)
+    grad_values = jnp.einsum(
+        "hqk,qhd->khd",
+        again_probs.astype(jnp.bfloat16),
+        grad_mixed,
+        preferred_element_type=jnp.float32,
+    )
+    grad_probs_attn = jnp.einsum(
+        "qhd,khd->hqk", grad_mixed, value_rows, preferred_element_type=jnp.float32
+    )
+    grad_scores = again_probs * (
+        grad_probs_attn - jnp.sum(again_probs * grad_probs_attn, axis=-1, keepdims=True)
+    )
+    grad_scores = grad_scores.astype(jnp.bfloat16)
+    grad_queries = (
+        jnp.einsum("hqk,khd->qhd", grad_scores, key_rows, preferred_element_type=jnp.float32)
+        * score_scale
+    )
+    grad_keys = (
+        jnp.einsum("hqk,qhd->khd", grad_scores, queries, preferred_element_type=jnp.float32)
+        * score_scale
+    )
+    grad_pre = jnp.stack(
+        [
+            rotate_backward(grad_queries, cosine_table, sine_table),
+            rotate_backward(grad_keys, cosine_table, sine_table),
+            grad_values,
+        ]
+    )
+    grad_pre = grad_pre.reshape(3, seq_rows, -1).astype(jnp.bfloat16)
+    low_one_part = jnp.einsum("cle,cde->ld", grad_pre, w_qkv, preferred_element_type=jnp.float32)
+    grad_norm_one = jnp.sum(low_one_part * unit_one, axis=0)
+    grad_low_one = lax.psum_scatter(
+        low_one_part.astype(jnp.bfloat16), "tp", scatter_dimension=0, tiled=True
+    ).astype(jnp.float32)
+    grad_bias = jnp.sum(grad_pre.astype(jnp.float32), axis=1).reshape(3, heads_here, head_dim)
+    grad_qkv = jnp.einsum("ld,cle->cde", low_one, grad_pre, preferred_element_type=jnp.float32)
+    grad_out_weight = contract(attn_mixed, grad_attn, 0, 0)
+    grad_input_norm, _ = rms_backward(grad_low_one, norm1_gain, mine(unit_one), mine(scale_one))
+    grad_tokens = grad_hidden + grad_input_norm
+
+    small = jnp.concatenate([grad_norm_one[None], small_sums[0] + small_sums[1]], axis=0)
+    small = lax.psum(small.reshape(-1, 128), ("ep", "tp")).reshape(small.shape)
+    small = lax.dynamic_slice_in_dim(
+        small, group_index * (features // groups), features // groups, 1
+    )
+    return (
+        output_rows,
+        grad_tokens,
+        small[0],
+        lax.psum_scatter(
+            grad_qkv.astype(jnp.bfloat16), "ep", scatter_dimension=1, tiled=True
+        ).astype(jnp.float32),
+        lax.psum_scatter(grad_bias, "ep", scatter_dimension=2, tiled=True),
+        lax.psum_scatter(
+            grad_out_weight.astype(jnp.bfloat16), "ep", scatter_dimension=1, tiled=True
+        ).astype(jnp.float32),
+        small[1],
+        small[3:].T,
+        small[2],
+        grad_shared_gu,
+        grad_shared_down,
+        grad_expert_gu[None],
+        grad_expert_down[None],
+    )
+
+
+def per_device(*arrays):
+    experts, chosen = arrays[6].shape[1], arrays[12].shape[1]
+    if experts <= 2 * chosen:
+        return dense_device(*arrays)
+    return routed_device(*arrays)
+
+
 def solution(mesh):
     return jax.shard_map(
         per_device,

time: 1870 us -> 1280 us (0.68)
  blocking collectives: 330 us -> 9.42 us
  local copies, waits for them, and re-layouts: 254 us -> 74.5 us
  Pallas kernels: 0 us -> 123 us
  matrix products: 219 us -> 124 us
  waiting for transfers between devices: 922 us -> 848 us
  other arithmetic: 107 us -> 63.2 us
    psum x3 -> x1, waiting for transfers between devices: 403 us -> 26.1 us  [dense_device(): small = lax.psum(small.reshape(-1, 128), ('ep', 'tp')).reshape(small.shape)]
    reduce_scatter x5 -> x13, waiting for transfers between devices: 267 us -> 598 us  [the longest x2 167 us: dense_device(): out_sum = lax.psum_scatter(out_part, 'ep', scatter_dimension=0, tiled=True)]
    all_to_all x2 -> x0, blocking collectives: 296 us -> none  [the longest x1 149 us: per_device(): lax.all_to_all(padded_two[slot_source], 'ep', split_axis=0, concat_axis=0...]
    all_gather x0 -> x6, waiting for transfers between devices: none -> 202 us  [the longest x2 143 us: dense_device(): rows_of.append(lax.all_gather(low_two, ('ep', 'tp'), axis=0, tiled=True))]
    all_to_all x2 -> x1, waiting for transfers between devices: 219 us -> 17.5 us  [dense_device(): lax.all_to_all(sent_shared.reshape(groups, features // groups, 3 * share)...]
    gather x6 -> x0, local copies, waits for them, and re-layouts: 126 us -> none  [the longest x1 27.7 us: per_device(): padded_two[slot_source]]
    pallas_call x0 -> x2, Pallas kernels: none -> 123 us  [expert_layer(): pl.pallas_call(functools.partial(expert_kernel, experts, expert_units, un...]
    dot_general x19 -> x13, matrix products: 147 us -> 41.4 us  [the longest x1 9.2 us: dense_device(): jnp.einsum('cle,cde->ld', grad_pre, w_qkv, preferred_element_type=jnp.flo...]
  transfers between devices with their start and end apart: 11 -> 22, of which waited for: 11 -> 19; matrix products, arithmetic and copies ran while one was open for 15% -> 15% of each run, Pallas kernels for 0% -> 10%
where the time goes in v1:
time: 1280 us
  waiting for transfers between devices  848 us (66%)
  matrix products  124 us (10%)
  Pallas kernels  123 us (10%)
  local copies, waits for them, and re-layouts  74.5 us (6%)
  other arithmetic  63.2 us (5%)
  between operations  16.9 us (1%)
  starting transfers between devices  16.4 us (1%)
    reduce_scatter x2, waiting for transfers between devices, dense_device(): out_sum = lax.psum_scatter(out_part, 'ep', scatter_dimension=0, tiled=True)  167 us
    all_gather x2, waiting for transfers between devices, dense_device(): rows_of.append(lax.all_gather(low_two, ('ep', 'tp'), axis=0, tiled=True))  143 us
    pallas_call x2, Pallas kernels, expert_layer(): pl.pallas_call(functools.partial(expert_kernel, experts, expert_units, un...  123 us
    reduce_scatter x2, waiting for transfers between devices, dense_device(): lax.psum_scatter(layer[half][1], 'ep', scatter_dimension=0, tiled=True)  113 us
    dot_general x14, matrix products, contract(): lax.dot_general(left_side, right_side, (((left_dim,), (right_dim,)), ((),...  80.9 us
    reduce_scatter x2, waiting for transfers between devices, dense_device(): grad_sum = lax.psum_scatter(grad_sum, 'tp', scatter_dimension=0, tiled=True)  61.8 us
    reduce_scatter x1, waiting for transfers between devices, dense_device(): lax.psum_scatter(grad_qkv.astype(jnp.bfloat16), 'ep', scatter_dimension=1...  59.5 us
    all_gather x2, waiting for transfers between devices, dense_device(): lax.all_gather(grad_hidden[half].astype(jnp.bfloat16), 'tp', axis=0, tile...  59.4 us
  transfers between devices with their start and end apart: 22, of which 19 were waited for; matrix products, arithmetic and copies ran while one was open for 15% of the time, Pallas kernels for 10%

profile of v1, /device:TPU:0, one launch (start us, length us, event | category | flops | bytes accessed | tf_op | source)
XLA Modules:
  0.0 1275.3 jit_solution(1881422253843464437)
XLA Ops:
  11.4 8.4 add_bitcast_fusion
  32.6 10.6 all-gather.13.cloned.1.call-start
  47.0 19.2 %reduce-scatter.19.cloned.1.call-done = bf16[80,2048]{1,0:T(8,128)(2,1)} async-done(((bf16[320,2048]{1,0:T(8,128)(2,1)}), bf16[80,2048]{1,0:T(8,128)(2,1)}) %reduce-scatter.19.cloned.1.call-update) | async-done | bytes 327696 | tf_op jit(solution)/shard_map/reduce_scatter | solution.py:558
  66.1 33.0 %reduce-scatter.17.cloned.1.call-done = bf16[80,2048]{1,0:T(8,128)(2,1)} async-done(((bf16[320,2048]{1,0:T(8,128)(2,1)}), bf16[80,2048]{1,0:T(8,128)(2,1)}) %reduce-scatter.17.cloned.1.call-update) | async-done | bytes 327696 | tf_op jit(solution)/shard_map/reduce_scatter | solution.py:558
  104.6 9.4 all_gather.23
  146.8 54.8 %all-gather.11.cloned.1.call-done.rows_ref = bf16[2560,2048]{1,0:T(8,128)(2,1)} async-done(((bf16[80,2048]{1,0:T(8,128)(2,1)}), bf16[2560,2048]{1,0:T(8,128)(2,1)}) %all-gather.11.cloned.1.call-update) | async-done | bytes 10485776 | tf_op jit(solution)/shard_map/all_gather | solution.py:564
  201.6 61.5 %shard_map.238 = (bf16[2560,2048]{1,0:T(8,128)(2,1)}, bf16[2560,2176]{1,0:T(8,128)(2,1)}, bf16[2560,640]{1,0:T(8,128)(2,1)}, bf16[2560,640]{1,0:T(8,128)(2,1)}, bf16[2560,640]{1,0:T(8,128)(2,1)}) custom-call(s32[1]{0:T(128)} %bitcast.9.index_ref, bf16[2560,2048]{1,0:T(8,128)(2,1)} %all-gather.11.cloned.1.call-done.rows_ref, ...), custom_call_target="tpu_custom_call" | custom-call | flops 40265318400 | bytes 41943040 | tf_op jit(solution)/shard_map/pallas_call | solution.py:432
  265.5 88.2 %all-gather.7.cloned.1.call-done.rows_ref = bf16[2560,2048]{1,0:T(8,128)(2,1)} async-done(((bf16[80,2048]{1,0:T(8,128)(2,1)}), bf16[2560,2048]{1,0:T(8,128)(2,1)}) %all-gather.7.cloned.1.call-update) | async-done | bytes 10485776 | tf_op jit(solution)/shard_map/all_gather | solution.py:564
  353.7 61.6 %shard_map.237 = (bf16[2560,2048]{1,0:T(8,128)(2,1)}, bf16[2560,2176]{1,0:T(8,128)(2,1)}, bf16[2560,640]{1,0:T(8,128)(2,1)}, bf16[2560,640]{1,0:T(8,128)(2,1)}, bf16[2560,640]{1,0:T(8,128)(2,1)}) custom-call(s32[1]{0:T(128)} %bitcast.9.index_ref, bf16[2560,2048]{1,0:T(8,128)(2,1)} %all-gather.7.cloned.1.call-done.rows_ref, ...), custom_call_target="tpu_custom_call" | custom-call | flops 40265318400 | bytes 41943040 | tf_op jit(solution)/shard_map/pallas_call | solution.py:432
  415.4 25.4 %reduce-scatter.21.cloned.1.call-done = bf16[320,2176]{1,0:T(8,128)(2,1)} async-done(((bf16[2560,2176]{1,0:T(8,128)(2,1)}), bf16[320,2176]{1,0:T(8,128)(2,1)}) %reduce-scatter.21.cloned.1.call-update) | async-done | bytes 1392656 | tf_op jit(solution)/shard_map/reduce_scatter | solution.py:585
  442.1 87.2 %reduce-scatter.31.cloned.1.call-done = bf16[320,2176]{1,0:T(8,128)(2,1)} async-done(((bf16[2560,2176]{1,0:T(8,128)(2,1)}), bf16[320,2176]{1,0:T(8,128)(2,1)}) %reduce-scatter.31.cloned.1.call-update) | async-done | bytes 1392656 | tf_op jit(solution)/shard_map/reduce_scatter | solution.py:585
  529.3 85.1 %reduce-scatter.27.cloned.1.call-done = bf16[320,2048]{1,0:T(8,128)(2,1)} async-done(((bf16[2560,2048]{1,0:T(8,128)(2,1)}), bf16[320,2048]{1,0:T(8,128)(2,1)}) %reduce-scatter.27.cloned.1.call-update) | async-done | bytes 1310736 | tf_op jit(solution)/shard_map/reduce_scatter | solution.py:627
  617.6 82.0 %reduce-scatter.23.cloned.1.call-done = bf16[320,2048]{1,0:T(8,128)(2,1)} async-done(((bf16[2560,2048]{1,0:T(8,128)(2,1)}), bf16[320,2048]{1,0:T(8,128)(2,1)}) %reduce-scatter.23.cloned.1.call-update) | async-done | bytes 1310736 | tf_op jit(solution)/shard_map/reduce_scatter | solution.py:627
  704.8 29.9 %reduce-scatter.35.cloned.1.call-done = bf16[80,2176]{1,0:T(8,128)(2,1)} async-done(((bf16[320,2176]{1,0:T(8,128)(2,1)}), bf16[80,2176]{1,0:T(8,128)(2,1)}) %reduce-scatter.35.cloned.1.call-update) | async-done | bytes 348176 | tf_op jit(solution)/shard_map/reduce_scatter | solution.py:587
  736.6 32.0 %reduce-scatter.33.cloned.1.call-done = bf16[80,2176]{1,0:T(8,128)(2,1)} async-done(((bf16[320,2176]{1,0:T(8,128)(2,1)}), bf16[80,2176]{1,0:T(8,128)(2,1)}) %reduce-scatter.33.cloned.1.call-update) | async-done | bytes 348176 | tf_op jit(solution)/shard_map/reduce_scatter | solution.py:587
  781.8 19.0 %reduce-scatter.29.cloned.1.call-done = bf16[80,2048]{1,0:T(8,128)(2,1)} async-done(((bf16[320,2048]{1,0:T(8,128)(2,1)}), bf16[80,2048]{1,0:T(8,128)(2,1)}) %reduce-scatter.29.cloned.1.call-update) | async-done | bytes 327696 | tf_op jit(solution)/shard_map/reduce_scatter | solution.py:628
  800.8 32.3 %reduce-scatter.25.cloned.1.call-done = bf16[80,2048]{1,0:T(8,128)(2,1)} async-done(((bf16[320,2048]{1,0:T(8,128)(2,1)}), bf16[80,2048]{1,0:T(8,128)(2,1)}) %reduce-scatter.25.cloned.1.call-update) | async-done | bytes 327696 | tf_op jit(solution)/shard_map/reduce_scatter | solution.py:628
  842.7 25.8 %all-gather.15.cloned.1.call-done = bf16[320,2048]{1,0:T(8,128)(2,1)} async-done(((bf16[80,2048]{1,0:T(8,128)(2,1)}), bf16[320,2048]{1,0:T(8,128)(2,1)}) %all-gather.15.cloned.1.call-update) | async-done | bytes 1310736 | tf_op jit(solution)/shard_map/all_gather | solution.py:612
  868.4 33.7 %all-gather.17.cloned.1.call-done = bf16[320,2048]{1,0:T(8,128)(2,1)} async-done(((bf16[80,2048]{1,0:T(8,128)(2,1)}), bf16[320,2048]{1,0:T(8,128)(2,1)}) %all-gather.17.cloned.1.call-update) | async-done | bytes 1310736 | tf_op jit(solution)/shard_map/all_gather | solution.py:612
  927.7 9.2 bitcast_convert_fusion
  951.0 11.2 fusion.56
  962.2 10.1 convolution_add_fusion.2
  974.6 11.1 fusion.54
  985.7 7.8 convert_bitcast_fusion
  993.5 12.1 convolution_add_fusion.1
  1008.0 11.3 fusion.55
  1019.3 9.6 convolution_add_fusion
  1046.9 17.5 %all-to-all-done = bf16[8,256,528]{1,2,0:T(8,128)(2,1)} async-done(((bf16[8,256,528]{1,2,0:T(8,128)(2,1)}), bf16[8,256,528]{1,2,0:T(8,128)(2,1)}, u32[]{:S(2)}, u32[]{:S(2)}) %all-to-all-start) | async-done | bytes 2162720 | tf_op jit(solution)/shard_map/all_to_all | solution.py:653
  1076.8 26.1 %all-reduce.2.cloned.1.call-done = f32[11,2048]{1,0:T(8,128)} async-done(((f32[11,2048]{1,0:T(8,128)}), f32[11,2048]{1,0:T(8,128)}) %all-reduce.2.cloned.1.call-update) | async-done | bytes 90128 | tf_op jit(solution)/shard_map/psum | solution.py:711
  1105.7 40.5 %reduce-scatter.41.cloned.1.call-done = bf16[512,256]{1,0:T(8,128)(2,1)} async-done(((bf16[512,2048]{1,0:T(8,128)(2,1)}), bf16[512,256]{1,0:T(8,128)(2,1)}) %reduce-scatter.41.cloned.1.call-update) | async-done | bytes 262160 | tf_op jit(solution)/shard_map/reduce_scatter | solution.py:723
  1148.0 52.8 %reduce-scatter.37.cloned.1.call-done = bf16[160,2048]{1,0:T(8,128)(2,1)} async-done(((bf16[640,2048]{1,0:T(8,128)(2,1)}), bf16[160,2048]{1,0:T(8,128)(2,1)}) %reduce-scatter.37.cloned.1.call-update) | async-done | bytes 655376 | tf_op jit(solution)/shard_map/reduce_scatter | solution.py:701
  1205.7 59.5 %reduce-scatter.39.cloned.1.call-done = bf16[3,256,512]{1,2,0:T(8,128)(2,1)} async-done(((bf16[3,2048,512]{1,2,0:T(8,128)(2,1)}), bf16[3,256,512]{1,2,0:T(8,128)(2,1)}) %reduce-scatter.39.cloned.1.call-update) | async-done | bytes 786448 | tf_op jit(solution)/shard_map/reduce_scatter | solution.py:719
  (289 shorter events, 180.7 us)
Async XLA Ops:
  8.0 58.1 %reduce-scatter.19.cloned.1.call-start = ((), (), s32[]{:S(2)}) async-start(), calls=%async_computation.18 | async-start | bytes 1638400 | tf_op jit(solution)/shard_map/reduce_scatter | solution.py:558
  31.9 67.2 %reduce-scatter.17.cloned.1.call-start = ((), (), s32[]{:S(2)}) async-start(), calls=%async_computation.15 | async-start | bytes 1638400 | tf_op jit(solution)/shard_map/reduce_scatter | solution.py:558
  32.6 114.2 %all-gather.13.cloned.1.call-start = ((), (), s32[]{:S(2)}) async-start(), calls=%async_computation.20 | async-start | bytes 11796480 | tf_op jit(solution)/shard_map/all_gather | solution.py:506
  46.9 67.3 %copy-start.34 = (bf16[2048]{0:T(1024)(128)(2,1)S(1)}, bf16[2048]{0:T(1024)(128)(2,1)}, u32[]{:S(2)}) copy-start(bf16[2048]{0:T(1024)(128)(2,1)} %param.21) | copy-start | bytes 12292
  46.9 68.4 %copy-start.29 = (bf16[2048,8]{0,1:T(8,128)(2,1)S(1)}, bf16[2048,8]{0,1:T(8,128)(2,1)}, u32[]{:S(2)}) copy-start(bf16[2048,8]{0,1:T(8,128)(2,1)} %param.20) | copy-start | bytes 98308
  46.9 154.7 %all-gather.11.cloned.1.call-start = ((), (), s32[]{:S(2)}) async-start(), calls=%async_computation.19 | async-start | bytes 10813440 | tf_op jit(solution)/shard_map/all_gather | solution.py:564
  103.2 162.4 %all-gather.9.cloned.1.call-start = ((), (), s32[]{:S(2)}) async-start(), calls=%async_computation.17 | async-start | bytes 11796480 | tf_op jit(solution)/shard_map/all_gather | solution.py:506
  103.8 249.9 %all-gather.7.cloned.1.call-start = ((), (), s32[]{:S(2)}) async-start(), calls=%async_computation.16 | async-start | bytes 10813440 | tf_op jit(solution)/shard_map/all_gather | solution.py:564
  104.5 336.3 %reduce-scatter.21.cloned.1.call-start = ((), (), s32[]{:S(2)}) async-start(), calls=%async_computation.21 | async-start | bytes 12533760 | tf_op jit(solution)/shard_map/reduce_scatter | solution.py:585
  263.2 266.1 %reduce-scatter.31.cloned.1.call-start = ((), (), s32[]{:S(2)}) async-start(), calls=%async_computation.26 | async-start | bytes 12533760 | tf_op jit(solution)/shard_map/reduce_scatter | solution.py:585
  415.3 199.1 %reduce-scatter.27.cloned.1.call-start = ((), (), s32[]{:S(2)}) async-start(), calls=%async_computation.24 | async-start | bytes 11796480 | tf_op jit(solution)/shard_map/reduce_scatter | solution.py:627
  440.8 258.9 %reduce-scatter.23.cloned.1.call-start = ((), (), s32[]{:S(2)}) async-start(), calls=%async_computation.22 | async-start | bytes 11796480 | tf_op jit(solution)/shard_map/reduce_scatter | solution.py:627
  441.4 293.3 %reduce-scatter.35.cloned.1.call-start = ((), (), s32[]{:S(2)}) async-start(), calls=%async_computation.28 | async-start | bytes 1740800 | tf_op jit(solution)/shard_map/reduce_scatter | solution.py:587
  442.0 257.8 %copy-start.35 = (bf16[2048]{0:T(1024)(128)(2,1)S(1)}, bf16[2048]{0:T(1024)(128)(2,1)}, u32[]{:S(2)}) copy-start(bf16[2048]{0:T(1024)(128)(2,1)} %param.21) | copy-start | bytes 12292
  442.0 260.4 %copy-start.5 = (bf16[80,2048]{1,0:T(8,128)(2,1)S(1)}, bf16[80,2048]{1,0:T(8,128)(2,1)}, u32[]{:S(2)}) copy-start(bf16[80,2048]{1,0:T(8,128)(2,1)} %get-tuple-element.140) | copy-start | bytes 983044
  442.0 260.4 %copy-start.30 = (bf16[2048,8]{0,1:T(8,128)(2,1)S(1)}, bf16[2048,8]{0,1:T(8,128)(2,1)}, u32[]{:S(2)}) copy-start(bf16[2048,8]{0,1:T(8,128)(2,1)} %param.20) | copy-start | bytes 98308
  442.0 326.5 %reduce-scatter.33.cloned.1.call-start = ((), (), s32[]{:S(2)}) async-start(), calls=%async_computation.27 | async-start | bytes 1740800 | tf_op jit(solution)/shard_map/reduce_scatter | solution.py:587
  529.3 174.1 %copy-start.4 = (bf16[80,2048]{1,0:T(8,128)(2,1)S(1)}, bf16[80,2048]{1,0:T(8,128)(2,1)}, u32[]{:S(2)}) copy-start(bf16[80,2048]{1,0:T(8,128)(2,1)} %get-tuple-element.139) | copy-start | bytes 983044
  529.3 271.5 %reduce-scatter.29.cloned.1.call-start = ((), (), s32[]{:S(2)}) async-start(), calls=%async_computation.25 | async-start | bytes 1638400 | tf_op jit(solution)/shard_map/reduce_scatter | solution.py:628
  614.5 218.6 %reduce-scatter.25.cloned.1.call-start = ((), (), s32[]{:S(2)}) async-start(), calls=%async_computation.23 | async-start | bytes 1638400 | tf_op jit(solution)/shard_map/reduce_scatter | solution.py:628
  617.6 159.6 %copy-start.11 = (bf16[80,2048]{1,0:T(8,128)(2,1)S(1)}, bf16[80,2048]{1,0:T(8,128)(2,1)}, u32[]{:S(2)}) copy-start(bf16[80,2048]{1,0:T(8,128)(2,1)} %reduce-scatter.19.cloned.1.call-done) | copy-start | bytes 983044
  617.6 159.6 %copy-start.37 = (f32[2048]{0:T(1024)S(1)}, f32[2048]{0:T(1024)}, u32[]{:S(2)}) copy-start(f32[2048]{0:T(1024)} %param.19) | copy-start | bytes 24580
  699.7 168.8 %all-gather.15.cloned.1.call-start = ((), (), s32[]{:S(2)}) async-start(), calls=%async_computation.29 | async-start | bytes 1638400 | tf_op jit(solution)/shard_map/all_gather | solution.py:612
  837.2 64.9 %all-gather.17.cloned.1.call-start = ((), (), s32[]{:S(2)}) async-start(), calls=%async_computation.30 | async-start | bytes 1638400 | tf_op jit(solution)/shard_map/all_gather | solution.py:612
  837.7 237.6 %reduce-scatter.43.cloned.1.call-start = ((), (), s32[]{:S(2)}) async-start(), calls=%async_computation.35 | async-start | bytes 73728
  937.9 165.0 %all-reduce.2.cloned.1.call-start = ((), (), s32[]{:S(2)}) async-start(), calls=%async_computation.32 | async-start | bytes 262144 | tf_op jit(solution)/shard_map/psum | solution.py:711
  945.1 201.2 %reduce-scatter.41.cloned.1.call-start = ((), (), s32[]{:S(2)}) async-start(), calls=%async_computation.34 | async-start | bytes 2359296 | tf_op jit(solution)/shard_map/reduce_scatter | solution.py:723
  950.1 250.7 %reduce-scatter.37.cloned.1.call-start = ((), (), s32[]{:S(2)}) async-start(), calls=%async_computation.31 | async-start | bytes 3276800 | tf_op jit(solution)/shard_map/reduce_scatter | solution.py:701
  950.9 314.3 %reduce-scatter.39.cloned.1.call-start = ((), (), s32[]{:S(2)}) async-start(), calls=%async_computation.33 | async-start | bytes 7077888 | tf_op jit(solution)/shard_map/reduce_scatter | solution.py:719
  1032.8 31.7 %all-to-all-start = ((bf16[8,256,528]{1,2,0:T(8,128)(2,1)}), bf16[8,256,528]{1,2,0:T(8,128)(2,1)}, u32[]{:S(2)}, u32[]{:S(2)}) async-start(bf16[8,256,528]{1,2,0:T(8,128)(2,1)} %pad_maximum_fusion.1), calls=%async_computation.13 | async-start | bytes 4325376 | tf_op jit(solution)/shard_map/all_to_all | solution.py:653
  1074.4 128.2 %copy-start.14 = (f32[80,2048]{1,0:T(8,128)S(1)}, f32[80,2048]{1,0:T(8,128)}, u32[]{:S(2)}) copy-start(f32[80,2048]{1,0:T(8,128)} %get-tuple-element.126) | copy-start | bytes 1966084
  1074.4 128.2 %copy-start.15 = (f32[80,2048]{1,0:T(8,128)S(1)}, f32[80,2048]{1,0:T(8,128)}, u32[]{:S(2)}) copy-start(f32[80,2048]{1,0:T(8,128)} %get-tuple-element.132) | copy-start | bytes 1966084
  (50 other events, 527.3 us)
Sparse Core Ops, SparseCore 0:
  32.0 34.0 reduce-scatter.18
  69.0 30.0 reduce-scatter.16
  837.3 31.1 all-gather.14
  870.4 31.6 all-gather.16
Sparse Core Ops, SparseCore 1:
  47.0 65.8 all-gather.12
  115.6 86.0 all-gather.10
  203.4 61.5 all-gather.8
  267.8 85.8 all-gather.6
  357.3 83.4 reduce-scatter.20
  444.4 84.8 reduce-scatter.30
  532.6 81.8 reduce-scatter.26
  617.8 81.8 reduce-scatter.22
  701.8 32.8 reduce-scatter.34
  737.0 31.4 reduce-scatter.32
  770.7 30.0 reduce-scatter.28
  803.1 29.9 reduce-scatter.24
  938.0 32.6 reduce-scatter.42
  976.8 126.0 all-reduce.1
  1106.2 40.0 reduce-scatter.40
  1148.6 52.2 reduce-scatter.36
  1204.2 60.9 reduce-scatter.38
